TPU v7x, 256 devices: a whole 4x4x8 slice. The times are simulated.
256 devices in a mesh: gx: 8 (over y, core), gy: 32 (over z, x).
Axes of the slice: x: 4, y: 4, z: 8, core: 2. Of those that a mesh axis runs over, the one named last changes fastest.
Arguments:
- pressure: float32 [512, 512, 512], P('gx', 'gy'), may hold values from -6 to 6
- divergence: float32 [512, 512, 512], P('gx', 'gy'), may hold values from -6 to 6
- diagonal: float32 [512, 512, 512], P('gx', 'gy'), may hold values from 0.05 to 0.5
- normals: float32 [3, 262144], P(None, ('gx', 'gy')), may hold values from -6 to 6
- traction: float32 [3, 262144], P(None, ('gx', 'gy')), may hold values from -3 to 3
- slot_of: int32 [8, 32768], P('gx'), may hold values from 0 to 98303, as said below
- counts: int32 [256], P(('gx', 'gy')), may hold values from 0 to 3072, as said below
- previous: float32 [3, 786432], P(None, ('gx', 'gy')), may hold values from -6 to 6
- secant_v: float32 [32, 3, 786432], P(None, None, ('gx', 'gy')), may hold values from -6 to 6
- secant_w: float32 [32, 3, 786432], P(None, None, ('gx', 'gy')), may hold values from -940.60406 to 940.60406
Outputs:
- pressure_new: float32 [512, 512, 512], P('gx', 'gy')
- coupled: float32 [3, 786432], P(None, ('gx', 'gy'))
Inputs may be any that keep to these rules, and one draw needn't show every extreme that they name: Within each group (row of slot_of) the places are distinct; place o * 3072 + s has s < counts[a * 32 + o]; every such place is used; the rows of one device (aligned blocks of 1024 entries) send at most 96 rows to one owner, and exactly 96 to some owner. The counts of one group sum to 32768; some owner of every group holds exactly 3072.
All inputs are finite; a program needn't handle non-finite values.
Results may differ from a plain program's by a relative error of at most 0.00019.
Values sent between devices are 32-bit elements; how exact they have to be, the bound alone decides.
A program may use at most 128 MiB of HBM per device.

v0:
```python
import jax
import jax.numpy as jnp
from jax import lax
from jax.sharding import PartitionSpec as P

SWEEPS = 2


def extended(cells, sides, width):
    for axis, dim in sides:
        count = lax.axis_size(axis)
        ends = count - 1
        head = lax.slice_in_dim(cells, 0, width, axis=dim)
        tail = lax.slice_in_dim(cells, cells.shape[dim] - width, cells.shape[dim], axis=dim)
        cells = jnp.concatenate(
            [
                lax.ppermute(tail, axis, [(i, (i + 1) % count) for i in range(ends)]),
                cells,
                lax.ppermute(head, axis, [((i + 1) % count, i) for i in range(ends)]),
            ],
            axis=dim,
        )
    return cells


def stencil_sum(padded):
    padded = jnp.pad(padded, ((0, 0), (0, 0), (1, 1)))
    total = padded[2:, 1:-1, 1:-1] + padded[:-2, 1:-1, 1:-1]
    total = total + padded[1:-1, 2:, 1:-1] + padded[1:-1, :-2, 1:-1]
    total = total + padded[1:-1, 1:-1, 2:] + padded[1:-1, 1:-1, :-2]
    return total


def sweep_once(field, divergence, diagonal):
    padded = extended(field, (("gx", 0), ("gy", 1)), 1)
    return (divergence + stencil_sum(padded)) / (6.0 + diagonal)


def shards(
    pressure, divergence, diagonal, normals, traction, slot_of, counts, previous, secant_v, secant_w
):
    columns = secant_v.shape[0]
    capacity = previous.shape[1]
    slot_index = jnp.arange(capacity, dtype=jnp.int32)
    occupied = (slot_index < counts[0]).astype(jnp.float32)
    masked_v = (secant_v * occupied[None, None, :]).reshape(columns, 3 * capacity)
    gram_local = jnp.dot(masked_v, masked_v.T, precision=lax.Precision.HIGHEST)
    field = pressure
    for sweep_index in range(SWEEPS):
        field = sweep_once(field, divergence, diagonal)
    surface = field[:, :, -1].reshape(-1)
    forces = normals * surface[None, :] + traction
    own_index = lax.axis_index("gy")
    all_slots = slot_of[0]
    gathered = lax.all_gather(forces, "gy", axis=1, tiled=True)
    placed = jnp.where(all_slots // capacity == own_index, all_slots % capacity, capacity)
    owned = jnp.zeros((3, capacity), jnp.float32).at[:, placed].set(gathered, mode="drop")
    residual = occupied[None, :] * (owned - previous)
    projection_local = jnp.dot(
        masked_v, residual.reshape(3 * capacity), precision=lax.Precision.HIGHEST
    )
    gram, projection = lax.psum((gram_local, projection_local), ("gx", "gy"))
    factor = jnp.linalg.cholesky(gram)
    coefficient = -jax.scipy.linalg.cho_solve((factor, True), projection)
    update = jnp.dot(
        coefficient, secant_w.reshape(columns, 3 * capacity), precision=lax.Precision.HIGHEST
    ).reshape(3, capacity)
    coupled = occupied[None, :] * (owned + update)
    return (field, coupled)


def solution(mesh):
    placed = (
        P("gx", "gy", None),
        P("gx", "gy", None),
        P("gx", "gy", None),
        P(None, ("gx", "gy")),
        P(None, ("gx", "gy")),
        P("gx", None),
        P(("gx", "gy")),
        P(None, ("gx", "gy")),
        P(None, None, ("gx", "gy")),
        P(None, None, ("gx", "gy")),
    )
    return jax.shard_map(
        shards,
        mesh=mesh,
        in_specs=placed,
        out_specs=(P("gx", "gy", None), P(None, ("gx", "gy"))),
        check_vma=False,
    )
```

profile of v0, /device:TPU:1, one launch (start us, length us, event | category | flops | bytes accessed | tf_op | source)
XLA Modules:
  0.0 306.0 jit_solution(7569810159518206231)
XLA Ops:
  0.6 0.0 copy-start
  0.6 0.9 fusion.35
  1.6 5.1 %collective-permute-start = (f32[1,16,512]{2,0,1:T(1,128)S(1)}, f32[1,16,512]{2,0,1:T(1,128)S(1)}, u32[]{:S(2)}, u32[]{:S(2)}) collective-permute-start(f32[1,16,512]{2,0,1:T(1,128)S(1)} %copy.23), channel_id=1, source_target_pairs={{32,0},{64,32},{96,64},{128,96},{160,128},{192,160},{224,192},{33,... | collective-permute-start | bytes 98312 | tf_op jit(solution)/shard_map/ppermute | solution.py:19
  6.7 1.9 collective-permute-start.1
  8.6 2.8 copy.24
  11.6 1.4 collective-permute-start.2
  13.0 4.0 %collective-permute-start.3 = (f32[66,1,512]{2,0,1:T(8,128)S(1)}, f32[66,1,512]{2,0,1:T(8,128)S(1)}, u32[]{:S(2)}, u32[]{:S(2)}) collective-permute-start(f32[66,1,512]{2,0,1:T(8,128)S(1)} %get-tuple-element.12), channel_id=1, source_target_pairs={{0,1},{1,2},{2,3},{3,4},{4,5},{5,6},{6,7},{7,8},{8,9},{9,10},{10,1... | collective-permute-start | bytes 405512 | tf_op jit(solution)/shard_map/ppermute | solution.py:17
  17.0 1.8 compare_select_fusion
  19.4 0.0 copy-start.2
  19.5 0.0 copy-start.4
  19.5 2.8 select_maximum_fusion.4
  22.4 0.0 copy-start.8
  22.4 6.9 %fusion.7 = f32[64,16,512]{2,0,1:T(8,128)S(1)} fusion(f32[66,18,514]{2,0,1:T(8,128)S(1)} %select_maximum_fusion.4, f32[66,1,512]{2,0,1:T(8,128)S(1)} %collective-permute-done.3, f32[1,16,512]{2,0,1:T(1,128)S(1)} %collective-permute-done, f32[64,16,512]{2,0,1:T(8,128)} %copy-done.1, f32[1,16,512]{2,0,1:T(1,128)S(1)} %collective-permute-done.1, ...), kind=kLoop, calls=%fused_computation.29 | loop fusion | flops 8388608 | bytes 12918784 | tf_op jit(solution)/shard_map/div | solution.py:36
  29.3 0.1 fusion.34
  29.3 3.4 %collective-permute-start.4 = (f32[1,16,512]{2,0,1:T(1,128)S(1)}, f32[1,16,512]{2,0,1:T(1,128)S(1)}, u32[]{:S(2)}, u32[]{:S(2)}) collective-permute-start(f32[1,16,512]{2,0,1:T(1,128)S(1)} %get-tuple-element.15), channel_id=1, source_target_pairs={{32,0},{64,32},{96,64},{128,96},{160,128},{192,160},{224,192},{33,... | collective-permute-start | bytes 98312 | tf_op jit(solution)/shard_map/ppermute | solution.py:19
  32.8 2.6 collective-permute-start.5
  35.4 1.7 copy.35
  37.1 1.4 collective-permute-start.6
  38.5 4.9 %collective-permute-start.7 = (f32[66,1,512]{2,0,1:T(8,128)S(1)}, f32[66,1,512]{2,0,1:T(8,128)S(1)}, u32[]{:S(2)}, u32[]{:S(2)}) collective-permute-start(f32[66,1,512]{2,0,1:T(8,128)S(1)} %get-tuple-element.10), channel_id=1, source_target_pairs={{0,1},{1,2},{2,3},{3,4},{4,5},{5,6},{6,7},{7,8},{8,9},{9,10},{10,1... | collective-permute-start | bytes 405512 | tf_op jit(solution)/shard_map/ppermute | solution.py:17
  43.5 1.1 convolution_bitcast_fusion
  44.5 0.0 copy-start.3
  44.6 1.1 collective-permute-done.6
  45.7 0.9 collective-permute-done.7
  46.6 2.8 select_maximum_fusion
  49.5 6.7 %fusion.2 = f32[64,16,512]{2,0,1:T(8,128)S(1)} fusion(f32[66,18,514]{2,0,1:T(8,128)S(1)} %select_maximum_fusion, f32[66,1,512]{2,0,1:T(8,128)S(1)} %collective-permute-done.7, f32[1,16,512]{2,0,1:T(1,128)S(1)} %collective-permute-done.4, f32[64,16,512]{2,0,1:T(8,128)S(1)} %fusion.7, f32[1,16,512]{2,0,1:T(1,128)S(1)} %collective-permute-done.5, ...), kind=kLoop, calls=%fused_computation.14 | loop fusion | flops 8388608 | bytes 12918784 | tf_op jit(solution)/shard_map/div | solution.py:36
  56.2 0.2 slice.128
  56.4 2.5 copy.37
  59.0 0.5 copy.31
  59.5 0.1 mul.33
  59.5 0.0 copy-done.10
  59.6 48.0 %all_gather.3 = f32[3,32768]{1,0:T(4,128)S(1)} all-gather(f32[3,1024]{1,0:T(4,128)S(1)} %multiply_add_fusion), channel_id=1, replica_groups=mesh['gx'=8,'gy'=32] {'gy'}, dimensions={1}, use_global_device_ids=true | all-gather | bytes 405504 | tf_op jit(solution)/shard_map/all_gather | solution.py:55
  107.6 8.5 %copy.32 = f32[32768,3]{1,0:T(8,128)} copy(f32[32768,3]{0,1:T(4,128)S(1)} %bitcast.77) | data formatting | bytes 786432 | tf_op jit(solution)/shard_map/all_gather | solution.py:55
  116.1 80.8 %scatter_custom_fusion = f32[3,3072]{0,1:T(8,128)S(1)} fusion(s32[32768]{0:T(1024)} %bitcast.78, f32[32768,3]{1,0:T(8,128)} %copy.32, f32[]{:T(128)} %constant.70.clone.1), kind=kCustom, calls=%fused_computation.58 | custom fusion | bytes 37376 | tf_op jit(solution)/shard_map/scatter | solution.py:57
  196.9 3.0 multiply_bitcast_fusion
  200.0 1.9 copy.40
  201.8 2.3 fusion.20
  204.1 86.8 %all-reduce.2 = (f32[32,32]{0,1:T(8,128)S(1)}, f32[32]{0:T(128)S(1)}) all-reduce(f32[32,32]{0,1:T(8,128)S(1)} %convolution_bitcast_fusion, f32[32]{0:T(128)S(1)} %fusion.20), channel_id=1, replica_groups=mesh['gx'=8,'gy'=32] {'gx','gy'}, use_global_device_ids=true, to_apply=%region_1.2 | all-reduce | flops 1056 | bytes 8448 | tf_op jit(solution)/shard_map/psum | solution.py:62
  291.0 0.1 copy.34
  291.1 2.9 cholesky.16
  294.0 0.6 compare_reduce_fusion
  294.7 0.7 fusion.28
  295.3 2.4 custom-call.10
  297.7 0.2 convolution_bitcast_fusion.2
  297.9 0.1 fusion.19
  298.1 0.7 fusion.12
  298.7 1.7 copy.42
  300.4 3.0 fusion.11
  303.5 2.5 copy.38
  (30 shorter events, 0.2 us)
Async XLA Ops:
  0.6 297.4 %copy-start = (f32[32,3,3072]{2,0,1:T(8,128)S(1)}, f32[32,3,3072]{2,0,1:T(8,128)}, u32[]{:S(2)}) copy-start(f32[32,3,3072]{2,0,1:T(8,128)} %param.19) | copy-start | bytes 3538948
  1.6 9.9 %collective-permute-start = (f32[1,16,512]{2,0,1:T(1,128)S(1)}, f32[1,16,512]{2,0,1:T(1,128)S(1)}, u32[]{:S(2)}, u32[]{:S(2)}) collective-permute-start(f32[1,16,512]{2,0,1:T(1,128)S(1)} %copy.23), channel_id=1, source_target_pairs={{32,0},{64,32},{96,64},{128,96},{160,128},{192,160},{224,192},{33,... | collective-permute-start | bytes 98312 | tf_op jit(solution)/shard_map/ppermute | solution.py:19
  6.7 4.8 %collective-permute-start.1 = (f32[1,16,512]{2,0,1:T(1,128)S(1)}, f32[1,16,512]{2,0,1:T(1,128)S(1)}, u32[]{:S(2)}, u32[]{:S(2)}) collective-permute-start(f32[1,16,512]{2,0,1:T(1,128)S(1)} %copy.25), channel_id=1, source_target_pairs={{0,32},{32,64},{64,96},{96,128},{128,160},{160,192},{192,224},{1,3... | collective-permute-start | bytes 98312 | tf_op jit(solution)/shard_map/ppermute | solution.py:17
  11.5 8.0 %copy-start.1 = (f32[64,16,512]{2,0,1:T(8,128)}, f32[64,16,512]{2,0,1:T(8,128)S(1)}, u32[]{:S(2)}) copy-start(f32[64,16,512]{2,0,1:T(8,128)S(1)} %copy.24) | copy-start | bytes 6291460
  11.5 5.5 %copy-start.7 = (s32[1,32768]{1,0:T(1,128)S(1)}, s32[1,32768]{1,0:T(1,128)}, u32[]{:S(2)}) copy-start(s32[1,32768]{1,0:T(1,128)} %param.15) | copy-start | bytes 393220
  11.6 7.9 %collective-permute-start.2 = (f32[66,1,512]{2,0,1:T(8,128)S(1)}, f32[66,1,512]{2,0,1:T(8,128)S(1)}, u32[]{:S(2)}, u32[]{:S(2)}) collective-permute-start(f32[66,1,512]{2,0,1:T(8,128)S(1)} %get-tuple-element.13), channel_id=1, source_target_pairs={{1,0},{2,1},{3,2},{4,3},{5,4},{6,5},{7,6},{8,7},{9,8},{10,9},{11,1... | collective-permute-start | bytes 405512 | tf_op jit(solution)/shard_map/ppermute | solution.py:19
  13.0 6.5 %collective-permute-start.3 = (f32[66,1,512]{2,0,1:T(8,128)S(1)}, f32[66,1,512]{2,0,1:T(8,128)S(1)}, u32[]{:S(2)}, u32[]{:S(2)}) collective-permute-start(f32[66,1,512]{2,0,1:T(8,128)S(1)} %get-tuple-element.12), channel_id=1, source_target_pairs={{0,1},{1,2},{2,3},{3,4},{4,5},{5,6},{6,7},{7,8},{8,9},{9,10},{10,1... | collective-permute-start | bytes 405512 | tf_op jit(solution)/shard_map/ppermute | solution.py:17
  19.4 2.9 copy-start.2
  19.5 2.9 copy-start.4
  22.4 13.0 %copy-start.8 = (f32[3,3072]{1,0:T(4,128)S(1)}, f32[3,3072]{1,0:T(4,128)}, u32[]{:S(2)}) copy-start(f32[3,3072]{1,0:T(4,128)} %param.17) | copy-start | bytes 110596
  29.3 7.7 %collective-permute-start.4 = (f32[1,16,512]{2,0,1:T(1,128)S(1)}, f32[1,16,512]{2,0,1:T(1,128)S(1)}, u32[]{:S(2)}, u32[]{:S(2)}) collective-permute-start(f32[1,16,512]{2,0,1:T(1,128)S(1)} %get-tuple-element.15), channel_id=1, source_target_pairs={{32,0},{64,32},{96,64},{128,96},{160,128},{192,160},{224,192},{33,... | collective-permute-start | bytes 98312 | tf_op jit(solution)/shard_map/ppermute | solution.py:19
  32.8 4.3 %collective-permute-start.5 = (f32[1,16,512]{2,0,1:T(1,128)S(1)}, f32[1,16,512]{2,0,1:T(1,128)S(1)}, u32[]{:S(2)}, u32[]{:S(2)}) collective-permute-start(f32[1,16,512]{2,0,1:T(1,128)S(1)} %get-tuple-element.14), channel_id=1, source_target_pairs={{0,32},{32,64},{64,96},{96,128},{128,160},{160,192},{192,224},{1,3... | collective-permute-start | bytes 98312 | tf_op jit(solution)/shard_map/ppermute | solution.py:17
  37.0 6.4 %copy-start.6 = (f32[32,3,3072]{2,0,1:T(8,128)S(1)}, f32[32,3,3072]{2,0,1:T(8,128)}, u32[]{:S(2)}) copy-start(f32[32,3,3072]{2,0,1:T(8,128)} %param.18) | copy-start | bytes 3538948
  37.1 8.6 %collective-permute-start.6 = (f32[66,1,512]{2,0,1:T(8,128)S(1)}, f32[66,1,512]{2,0,1:T(8,128)S(1)}, u32[]{:S(2)}, u32[]{:S(2)}) collective-permute-start(f32[66,1,512]{2,0,1:T(8,128)S(1)} %get-tuple-element.11), channel_id=1, source_target_pairs={{1,0},{2,1},{3,2},{4,3},{5,4},{6,5},{7,6},{8,7},{9,8},{10,9},{11,1... | collective-permute-start | bytes 405512 | tf_op jit(solution)/shard_map/ppermute | solution.py:19
  38.5 8.1 %collective-permute-start.7 = (f32[66,1,512]{2,0,1:T(8,128)S(1)}, f32[66,1,512]{2,0,1:T(8,128)S(1)}, u32[]{:S(2)}, u32[]{:S(2)}) collective-permute-start(f32[66,1,512]{2,0,1:T(8,128)S(1)} %get-tuple-element.10), channel_id=1, source_target_pairs={{0,1},{1,2},{2,3},{3,4},{4,5},{5,6},{6,7},{7,8},{8,9},{9,10},{10,1... | collective-permute-start | bytes 405512 | tf_op jit(solution)/shard_map/ppermute | solution.py:17
  44.5 4.9 %copy-start.3 = (f32[64,16,512]{2,1,0:T(8,128)S(1)}, f32[64,16,512]{2,1,0:T(8,128)}, u32[]{:S(2)}) copy-start(f32[64,16,512]{2,1,0:T(8,128)} %param.11) | copy-start | bytes 6291460
  44.6 4.9 %copy-start.5 = (f32[64,16,512]{2,1,0:T(8,128)S(1)}, f32[64,16,512]{2,1,0:T(8,128)}, u32[]{:S(2)}) copy-start(f32[64,16,512]{2,1,0:T(8,128)} %param.12) | copy-start | bytes 6291460
  56.4 3.1 %copy-start.9 = (f32[3,1024]{1,0:T(4,128)S(1)}, f32[3,1024]{1,0:T(4,128)}, u32[]{:S(2)}) copy-start(f32[3,1024]{1,0:T(4,128)} %param.14) | copy-start | bytes 36868
  56.4 3.1 %copy-start.10 = (f32[3,1024]{1,0:T(4,128)S(1)}, f32[3,1024]{1,0:T(4,128)}, u32[]{:S(2)}) copy-start(f32[3,1024]{1,0:T(4,128)} %param.13) | copy-start | bytes 36868
where the time goes:
time: 307 us; the launch traced here: 306 us
  blocking collectives  135 us (44%)
  local copies, waits for them, and re-layouts  104 us (34%)
  other arithmetic  33.9 us (11%)
  starting transfers between devices  24.8 us (8%)
  matrix products  4.35 us (1%)
    psum x1, blocking collectives, shards(): gram, projection = lax.psum((gram_local, projection_local), ('gx', 'gy'))  86.8 us
    scatter x1, local copies, waits for them, and re-layouts, shards(): jnp.zeros((3, capacity), jnp.float32).at[:, placed]  80.8 us
    all_gather x1, blocking collectives, shards(): gathered = lax.all_gather(forces, 'gy', axis=1, tiled=True)  48 us
    div x2, other arithmetic, sweep_once(): return (divergence + stencil_sum(padded)) / (6.0 + diagonal)  13.6 us
    ppermute x4, starting transfers between devices, extended(): lax.ppermute(tail, axis, [(i, (i + 1) % count) for i in range(ends)])  13.4 us
    ppermute x4, starting transfers between devices, extended(): lax.ppermute(head, axis, [((i + 1) % count, i) for i in range(ends)])  11.4 us
    unnamed x26, local copies, waits for them, and re-layouts  9.59 us
    all_gather x1, local copies, waits for them, and re-layouts, shards(): gathered = lax.all_gather(forces, 'gy', axis=1, tiled=True)  8.53 us
  transfers between devices with their start and end apart: 8, of which 2 were waited for; matrix products, arithmetic and copies ran while one was open for 2% of the time, Pallas kernels for 0%

commit v1 on v0

--- a/solution.py
+++ b/solution.py
@@ -4,6 +4,18 @@
 from jax.sharding import PartitionSpec as P
 
 SWEEPS = 2
+
+
+def gather_by_bits(x, axis, dim):
+    ways, here, hop = (lax.axis_size(axis), lax.axis_index(axis), x.shape[dim])
+    line, have = (x, 1)
+    while have < ways:
+        line = jnp.concatenate(
+            [line, lax.ppermute(line, axis, [(d, (d - have) % ways) for d in range(ways)])],
+            axis=dim,
+        )
+        have = 2 * have
+    return jnp.roll(line, here * hop, axis=dim)
 
 
 def extended(cells, sides, width):
@@ -52,7 +64,7 @@
     forces = normals * surface[None, :] + traction
     own_index = lax.axis_index("gy")
     all_slots = slot_of[0]
-    gathered = lax.all_gather(forces, "gy", axis=1, tiled=True)
+    gathered = gather_by_bits(forces, "gy", 1)
     placed = jnp.where(all_slots // capacity == own_index, all_slots % capacity, capacity)
     owned = jnp.zeros((3, capacity), jnp.float32).at[:, placed].set(gathered, mode="drop")
     residual = occupied[None, :] * (owned - previous)

time: 307 us -> 300 us (0.977)
  blocking collectives: 135 us -> 88 us
  starting transfers between devices: 24.8 us -> 49.3 us
  waiting for transfers between devices: 2.07 us -> 8.8 us
  local copies, waits for them, and re-layouts: 104 us -> 110 us
    all_gather x1 -> x0, blocking collectives: 48 us -> none  [shards(): gathered = lax.all_gather(forces, 'gy', axis=1, tiled=True)]
    ppermute x0 -> x5, starting transfers between devices: none -> 24.4 us  [gather_by_bits(): lax.ppermute(line, axis, [(d, (d - have) % ways) for d in range(ways)])]
    dynamic_slice x0 -> x2, local copies, waits for them, and re-layouts: none -> 8.59 us  [gather_by_bits(): return jnp.roll(line, here * hop, axis=dim)]
    all_gather x1 -> x0, local copies, waits for them, and re-layouts: 8.53 us -> none  [shards(): gathered = lax.all_gather(forces, 'gy', axis=1, tiled=True)]
    unnamed x26 -> x56, local copies, waits for them, and re-layouts: 9.59 us -> 14.4 us
    ppermute x0 -> x5, waiting for transfers between devices: none -> 4.58 us  [gather_by_bits(): lax.ppermute(line, axis, [(d, (d - have) % ways) for d in range(ways)])]
  transfers between devices with their start and end apart: 8 -> 13, of which waited for: 2 -> 8; matrix products, arithmetic and copies ran while one was open for 2% -> 5% of each run, Pallas kernels for 0% -> 0%
where the time goes in v1:
time: 300 us
  local copies, waits for them, and re-layouts  110 us (37%)
  blocking collectives  88 us (29%)
  starting transfers between devices  49.3 us (16%)
  other arithmetic  35.1 us (12%)
  waiting for transfers between devices  8.8 us (3%)
  matrix products  6.78 us (2%)
    psum x1, blocking collectives, shards(): gram, projection = lax.psum((gram_local, projection_local), ('gx', 'gy'))  88 us
    scatter x1, local copies, waits for them, and re-layouts, shards(): jnp.zeros((3, capacity), jnp.float32).at[:, placed]  80.8 us
    ppermute x5, starting transfers between devices, gather_by_bits(): lax.ppermute(line, axis, [(d, (d - have) % ways) for d in range(ways)])  24.4 us
    unnamed x56, local copies, waits for them, and re-layouts  14.4 us
    ppermute x4, starting transfers between devices, extended(): lax.ppermute(tail, axis, [(i, (i + 1) % count) for i in range(ends)])  13.7 us
    div x2, other arithmetic, sweep_once(): return (divergence + stencil_sum(padded)) / (6.0 + diagonal)  13.5 us
    ppermute x4, starting transfers between devices, extended(): lax.ppermute(head, axis, [((i + 1) % count, i) for i in range(ends)])  11.2 us
    dynamic_slice x2, local copies, waits for them, and re-layouts, gather_by_bits(): return jnp.roll(line, here * hop, axis=dim)  8.59 us
  transfers between devices with their start and end apart: 13, of which 8 were waited for; matrix products, arithmetic and copies ran while one was open for 5% of the time, Pallas kernels for 0%

profile of v1, /device:TPU:1, one launch (start us, length us, event | category | flops | bytes accessed | tf_op | source)
XLA Modules:
  0.0 299.8 jit_solution(8713053610088804036)
XLA Ops:
  0.6 0.9 fusion.35
  1.6 5.1 %collective-permute-start = (f32[1,16,512]{2,0,1:T(1,128)S(1)}, f32[1,16,512]{2,0,1:T(1,128)S(1)}, u32[]{:S(2)}, u32[]{:S(2)}) collective-permute-start(f32[1,16,512]{2,0,1:T(1,128)S(1)} %copy.23), channel_id=1, source_target_pairs={{32,0},{64,32},{96,64},{128,96},{160,128},{192,160},{224,192},{33,... | collective-permute-start | bytes 98312 | tf_op jit(solution)/shard_map/ppermute | solution.py:31
  6.7 1.9 collective-permute-start.1
  8.6 2.8 copy.24
  11.5 1.3 collective-permute-start.2
  12.8 4.3 %collective-permute-start.3 = (f32[66,1,512]{2,0,1:T(8,128)S(1)}, f32[66,1,512]{2,0,1:T(8,128)S(1)}, u32[]{:S(2)}, u32[]{:S(2)}) collective-permute-start(f32[66,1,512]{2,0,1:T(8,128)S(1)} %get-tuple-element.14), channel_id=1, source_target_pairs={{0,1},{1,2},{2,3},{3,4},{4,5},{5,6},{6,7},{7,8},{8,9},{9,10},{10,1... | collective-permute-start | bytes 405512 | tf_op jit(solution)/shard_map/ppermute | solution.py:29
  17.1 1.2 collective-permute-done.2
  18.3 1.2 collective-permute-done.3
  19.5 2.8 select_maximum_fusion.4
  22.4 6.8 %fusion.7 = f32[64,16,512]{2,0,1:T(8,128)S(1)} fusion(f32[66,18,514]{2,0,1:T(8,128)S(1)} %select_maximum_fusion.4, f32[66,1,512]{2,0,1:T(8,128)S(1)} %collective-permute-done.3, f32[1,16,512]{2,0,1:T(1,128)S(1)} %collective-permute-done, f32[64,16,512]{2,0,1:T(8,128)S(1)} %copy.24, f32[1,16,512]{2,0,1:T(1,128)S(1)} %collective-permute-done.1, ...), kind=kLoop, calls=%fused_computation.29 | loop fusion | flops 8388608 | bytes 12918784 | tf_op jit(solution)/shard_map/div | solution.py:48
  29.3 3.5 %collective-permute-start.4 = (f32[1,16,512]{2,0,1:T(1,128)S(1)}, f32[1,16,512]{2,0,1:T(1,128)S(1)}, u32[]{:S(2)}, u32[]{:S(2)}) collective-permute-start(f32[1,16,512]{2,0,1:T(1,128)S(1)} %get-tuple-element.17), channel_id=1, source_target_pairs={{32,0},{64,32},{96,64},{128,96},{160,128},{192,160},{224,192},{33,... | collective-permute-start | bytes 98312 | tf_op jit(solution)/shard_map/ppermute | solution.py:31
  32.8 2.6 collective-permute-start.5
  35.4 1.0 collective-permute-done.5
  36.4 1.3 collective-permute-start.6
  37.7 4.9 %collective-permute-start.7 = (f32[66,1,512]{2,0,1:T(8,128)S(1)}, f32[66,1,512]{2,0,1:T(8,128)S(1)}, u32[]{:S(2)}, u32[]{:S(2)}) collective-permute-start(f32[66,1,512]{2,0,1:T(8,128)S(1)} %get-tuple-element.12), channel_id=1, source_target_pairs={{0,1},{1,2},{2,3},{3,4},{4,5},{5,6},{6,7},{7,8},{8,9},{9,10},{10,1... | collective-permute-start | bytes 405512 | tf_op jit(solution)/shard_map/ppermute | solution.py:29
  42.7 1.8 compare_select_fusion
  45.2 0.8 collective-permute-done.7
  46.0 2.8 select_maximum_fusion
  48.9 6.7 %fusion.2 = f32[64,16,512]{2,0,1:T(8,128)S(1)} fusion(f32[66,18,514]{2,0,1:T(8,128)S(1)} %select_maximum_fusion, f32[66,1,512]{2,0,1:T(8,128)S(1)} %collective-permute-done.7, f32[1,16,512]{2,0,1:T(1,128)S(1)} %collective-permute-done.4, f32[64,16,512]{2,0,1:T(8,128)S(1)} %fusion.7, f32[1,16,512]{2,0,1:T(1,128)S(1)} %collective-permute-done.5, ...), kind=kLoop, calls=%fused_computation.14 | loop fusion | flops 8388608 | bytes 12918784 | tf_op jit(solution)/shard_map/div | solution.py:48
  55.6 1.3 copy-done.1
  58.3 9.1 %collective-permute-start.8 = (f32[3,1024]{1,0:T(4,128)S(1)}, f32[3,1024]{1,0:T(4,128)S(1)}, u32[]{:S(2)}, u32[]{:S(2)}) collective-permute-start(f32[3,1024]{1,0:T(4,128)S(1)} %get-tuple-element.11), channel_id=1, source_target_pairs={{0,31},{1,0},{2,1},{3,2},{4,3},{5,4},{6,5},{7,6},{8,7},{9,8},{10,9... | collective-permute-start | bytes 36872 | tf_op jit(solution)/shard_map/ppermute | solution.py:14
  68.3 5.1 %collective-permute-start.9 = (f32[3,2048]{1,0:T(4,128)S(1)}, f32[3,2048]{1,0:T(4,128)S(1)}, u32[]{:S(2)}, u32[]{:S(2)}) collective-permute-start(f32[3,2048]{1,0:T(4,128)S(1)} %pad_maximum_fusion.24), channel_id=1, source_target_pairs={{0,30},{1,31},{2,0},{3,1},{4,2},{5,3},{6,4},{7,5},{8,6},{9,7},{10,... | collective-permute-start | bytes 73736 | tf_op jit(solution)/shard_map/ppermute | solution.py:14
  73.4 0.6 constant_dynamic-update-slice_fusion.3
  74.4 3.8 %collective-permute-start.10 = (f32[3,4096]{1,0:T(4,128)S(1)}, f32[3,4096]{1,0:T(4,128)S(1)}, u32[]{:S(2)}, u32[]{:S(2)}) collective-permute-start(f32[3,4096]{1,0:T(4,128)S(1)} %pad_maximum_fusion.23), channel_id=1, source_target_pairs={{0,28},{1,29},{2,30},{3,31},{4,0},{5,1},{6,2},{7,3},{8,4},{9,5},{1... | collective-permute-start | bytes 147464 | tf_op jit(solution)/shard_map/ppermute | solution.py:14
  78.3 0.6 constant_dynamic-update-slice_fusion.2
  78.9 0.7 collective-permute-done.10
  79.6 2.3 collective-permute-start.11
  82.0 0.7 constant_dynamic-update-slice_fusion.1
  82.6 3.2 %collective-permute-done.11 = f32[3,8192]{1,0:T(4,128)S(1)} collective-permute-done((f32[3,8192]{1,0:T(4,128)S(1)}, f32[3,8192]{1,0:T(4,128)S(1)}, u32[]{:S(2)}, u32[]{:S(2)}) %collective-permute-start.11) | collective-permute-done | bytes 98336 | tf_op jit(solution)/shard_map/ppermute | solution.py:14
  85.8 0.7 constant_dynamic-update-slice_fusion
  86.6 4.1 %collective-permute-start.12 = (f32[3,16384]{1,0:T(4,128)}, f32[3,16384]{1,0:T(4,128)S(1)}, u32[]{:S(2)}, u32[]{:S(2)}) collective-permute-start(f32[3,16384]{1,0:T(4,128)} %get-tuple-element.20), channel_id=1, source_target_pairs={{0,16},{1,17},{2,18},{3,19},{4,20},{5,21},{6,22},{7,23},{8,24},{9,... | collective-permute-start | bytes 589832 | tf_op jit(solution)/shard_map/ppermute | solution.py:14
  91.2 2.5 copy.35
  93.7 3.5 %convolution_bitcast_fusion = f32[32,32]{0,1:T(8,128)} fusion(f32[32,3,3072]{2,0,1:T(8,128)} %param.18, f32[3072]{0:T(1024)} %fusion.32), kind=kOutput, calls=%fused_computation.49 | convolution fusion | flops 113541120 | bytes 1196032 | tf_op jit(solution)/shard_map/dot_general | solution.py:59
  97.3 2.5 copy.37
  100.2 8.5 %copy.32 = f32[32768,3]{1,0:T(8,128)} copy(f32[32768,3]{0,1:T(4,128)S(1)} %dynamic-slice_bitcast_fusion) | data formatting | bytes 786432 | tf_op jit(solution)/shard_map/jit(_roll_dynamic)/dynamic_slice | solution.py:18
  108.7 80.8 %scatter_custom_fusion = f32[3,3072]{0,1:T(8,128)S(1)} fusion(s32[32768]{0:T(1024)} %bitcast.78, f32[32768,3]{1,0:T(8,128)} %copy.32, f32[]{:T(128)} %constant.89.clone.1), kind=kCustom, calls=%fused_computation.58 | custom fusion | bytes 37376 | tf_op jit(solution)/shard_map/scatter | solution.py:69
  189.5 3.1 %multiply_bitcast_fusion = f32[3,3072,1]{0,1,2:T(8,128)} fusion(f32[3,3072]{0,1:T(8,128)S(1)} %scatter_custom_fusion, f32[3,3072]{0,1:T(8,128)} %copy.35, f32[3072]{0:T(1024)S(1)} %copy-done.15), kind=kLoop, calls=%fused_computation.45 | loop fusion | flops 18432 | bytes 122880 | tf_op jit(solution)/shard_map/mul | solution.py:70
  192.6 1.9 copy.40
  194.5 2.3 fusion.20
  196.8 88.0 %all-reduce.2 = (f32[32,32]{0,1:T(8,128)S(1)}, f32[32]{0:T(128)S(1)}) all-reduce(f32[32,32]{0,1:T(8,128)S(1)} %copy-done.18, f32[32]{0:T(128)S(1)} %fusion.20), channel_id=1, replica_groups=mesh['gx'=8,'gy'=32] {'gx','gy'}, use_global_device_ids=true, to_apply=%region_1.2 | all-reduce | flops 1056 | bytes 8448 | tf_op jit(solution)/shard_map/psum | solution.py:74
  284.8 2.9 cholesky.16
  287.8 0.6 compare_reduce_fusion
  288.4 0.7 fusion.28
  289.1 2.4 custom-call.10
  291.8 0.7 fusion.12
  292.5 1.7 copy.42
  294.2 3.1 %fusion.11 = f32[3,3072]{0,1:T(8,128)} fusion(f32[3,3072]{0,1:T(8,128)S(1)} %scatter_custom_fusion, f32[1,3,3072]{1,2,0:T(8,128)} %copy.42, f32[3072]{0:T(1024)S(1)} %copy-done.15), kind=kLoop, calls=%fused_computation.44 | loop fusion | flops 18432 | bytes 122880 | tf_op jit(solution)/shard_map/mul | solution.py:80
  297.3 2.5 copy.38
  (75 shorter events, 4.3 us)
Async XLA Ops:
  0.6 291.2 %copy-start = (f32[32,3,3072]{2,0,1:T(8,128)S(1)}, f32[32,3,3072]{2,0,1:T(8,128)}, u32[]{:S(2)}) copy-start(f32[32,3,3072]{2,0,1:T(8,128)} %param.19) | copy-start | bytes 3538948
  1.6 9.9 %collective-permute-start = (f32[1,16,512]{2,0,1:T(1,128)S(1)}, f32[1,16,512]{2,0,1:T(1,128)S(1)}, u32[]{:S(2)}, u32[]{:S(2)}) collective-permute-start(f32[1,16,512]{2,0,1:T(1,128)S(1)} %copy.23), channel_id=1, source_target_pairs={{32,0},{64,32},{96,64},{128,96},{160,128},{192,160},{224,192},{33,... | collective-permute-start | bytes 98312 | tf_op jit(solution)/shard_map/ppermute | solution.py:31
  6.7 4.8 %collective-permute-start.1 = (f32[1,16,512]{2,0,1:T(1,128)S(1)}, f32[1,16,512]{2,0,1:T(1,128)S(1)}, u32[]{:S(2)}, u32[]{:S(2)}) collective-permute-start(f32[1,16,512]{2,0,1:T(1,128)S(1)} %copy.25), channel_id=1, source_target_pairs={{0,32},{32,64},{64,96},{96,128},{128,160},{160,192},{192,224},{1,3... | collective-permute-start | bytes 98312 | tf_op jit(solution)/shard_map/ppermute | solution.py:29
  11.5 6.8 %collective-permute-start.2 = (f32[66,1,512]{2,0,1:T(8,128)S(1)}, f32[66,1,512]{2,0,1:T(8,128)S(1)}, u32[]{:S(2)}, u32[]{:S(2)}) collective-permute-start(f32[66,1,512]{2,0,1:T(8,128)S(1)} %get-tuple-element.15), channel_id=1, source_target_pairs={{1,0},{2,1},{3,2},{4,3},{5,4},{6,5},{7,6},{8,7},{9,8},{10,9},{11,1... | collective-permute-start | bytes 405512 | tf_op jit(solution)/shard_map/ppermute | solution.py:31
  12.8 9.5 %copy-start.3 = (f32[64,16,512]{2,1,0:T(8,128)S(1)}, f32[64,16,512]{2,1,0:T(8,128)}, u32[]{:S(2)}) copy-start(f32[64,16,512]{2,1,0:T(8,128)} %param.11) | copy-start | bytes 6291460
  12.8 9.5 %copy-start.5 = (f32[64,16,512]{2,1,0:T(8,128)S(1)}, f32[64,16,512]{2,1,0:T(8,128)}, u32[]{:S(2)}) copy-start(f32[64,16,512]{2,1,0:T(8,128)} %param.12) | copy-start | bytes 6291460
  12.8 6.7 %collective-permute-start.3 = (f32[66,1,512]{2,0,1:T(8,128)S(1)}, f32[66,1,512]{2,0,1:T(8,128)S(1)}, u32[]{:S(2)}, u32[]{:S(2)}) collective-permute-start(f32[66,1,512]{2,0,1:T(8,128)S(1)} %get-tuple-element.14), channel_id=1, source_target_pairs={{0,1},{1,2},{2,3},{3,4},{4,5},{5,6},{6,7},{7,8},{8,9},{9,10},{10,1... | collective-permute-start | bytes 405512 | tf_op jit(solution)/shard_map/ppermute | solution.py:29
  29.2 13.5 %copy-start.17 = (s32[1,32768]{1,0:T(1,128)S(1)}, s32[1,32768]{1,0:T(1,128)}, u32[]{:S(2)}) copy-start(s32[1,32768]{1,0:T(1,128)} %param.15) | copy-start | bytes 393220
  29.3 6.1 %collective-permute-start.4 = (f32[1,16,512]{2,0,1:T(1,128)S(1)}, f32[1,16,512]{2,0,1:T(1,128)S(1)}, u32[]{:S(2)}, u32[]{:S(2)}) collective-permute-start(f32[1,16,512]{2,0,1:T(1,128)S(1)} %get-tuple-element.17), channel_id=1, source_target_pairs={{32,0},{64,32},{96,64},{128,96},{160,128},{192,160},{224,192},{33,... | collective-permute-start | bytes 98312 | tf_op jit(solution)/shard_map/ppermute | solution.py:31
  32.8 3.6 %collective-permute-start.5 = (f32[1,16,512]{2,0,1:T(1,128)S(1)}, f32[1,16,512]{2,0,1:T(1,128)S(1)}, u32[]{:S(2)}, u32[]{:S(2)}) collective-permute-start(f32[1,16,512]{2,0,1:T(1,128)S(1)} %get-tuple-element.16), channel_id=1, source_target_pairs={{0,32},{32,64},{64,96},{96,128},{128,160},{160,192},{192,224},{1,3... | collective-permute-start | bytes 98312 | tf_op jit(solution)/shard_map/ppermute | solution.py:29
  36.4 8.7 %collective-permute-start.6 = (f32[66,1,512]{2,0,1:T(8,128)S(1)}, f32[66,1,512]{2,0,1:T(8,128)S(1)}, u32[]{:S(2)}, u32[]{:S(2)}) collective-permute-start(f32[66,1,512]{2,0,1:T(8,128)S(1)} %get-tuple-element.13), channel_id=1, source_target_pairs={{1,0},{2,1},{3,2},{4,3},{5,4},{6,5},{7,6},{8,7},{9,8},{10,9},{11,1... | collective-permute-start | bytes 405512 | tf_op jit(solution)/shard_map/ppermute | solution.py:31
  37.7 8.2 %collective-permute-start.7 = (f32[66,1,512]{2,0,1:T(8,128)S(1)}, f32[66,1,512]{2,0,1:T(8,128)S(1)}, u32[]{:S(2)}, u32[]{:S(2)}) collective-permute-start(f32[66,1,512]{2,0,1:T(8,128)S(1)} %get-tuple-element.12), channel_id=1, source_target_pairs={{0,1},{1,2},{2,3},{3,4},{4,5},{5,6},{6,7},{7,8},{8,9},{9,10},{10,1... | collective-permute-start | bytes 405512 | tf_op jit(solution)/shard_map/ppermute | solution.py:29
  45.1 3.7 %copy-start.4 = (f32[64,16,512]{2,1,0:T(8,128)S(1)}, f32[64,16,512]{2,1,0:T(8,128)}, u32[]{:S(2)}) copy-start(f32[64,16,512]{2,1,0:T(8,128)} %param.11) | copy-start | bytes 6291460
  45.1 3.7 %copy-start.6 = (f32[64,16,512]{2,1,0:T(8,128)S(1)}, f32[64,16,512]{2,1,0:T(8,128)}, u32[]{:S(2)}) copy-start(f32[64,16,512]{2,1,0:T(8,128)} %param.12) | copy-start | bytes 6291460
  48.8 8.8 %copy-start.19 = (f32[3,1024]{1,0:T(4,128)S(1)}, f32[3,1024]{1,0:T(4,128)}, u32[]{:S(2)}) copy-start(f32[3,1024]{1,0:T(4,128)} %param.14) | copy-start | bytes 36868
  48.8 8.8 %copy-start.20 = (f32[3,1024]{1,0:T(4,128)S(1)}, f32[3,1024]{1,0:T(4,128)}, u32[]{:S(2)}) copy-start(f32[3,1024]{1,0:T(4,128)} %param.13) | copy-start | bytes 36868
  55.6 1.3 copy-start.1
  57.7 39.5 %copy-start.2 = (f32[64,16,512]{2,0,1:T(8,128)S(1)}, f32[64,16,512]{2,0,1:T(8,128)}, u32[]{:S(2)}) copy-start(f32[64,16,512]{2,0,1:T(8,128)} %copy-done.1) | copy-start | bytes 6291460
  58.3 10.0 %collective-permute-start.8 = (f32[3,1024]{1,0:T(4,128)S(1)}, f32[3,1024]{1,0:T(4,128)S(1)}, u32[]{:S(2)}, u32[]{:S(2)}) collective-permute-start(f32[3,1024]{1,0:T(4,128)S(1)} %get-tuple-element.11), channel_id=1, source_target_pairs={{0,31},{1,0},{2,1},{3,2},{4,3},{5,4},{6,5},{7,6},{8,7},{9,8},{10,9... | collective-permute-start | bytes 36872 | tf_op jit(solution)/shard_map/ppermute | solution.py:14
  68.3 11.3 %copy-start.13 = (f32[3,1024]{1,0:T(4,128)}, f32[3,1024]{1,0:T(4,128)S(1)}, u32[]{:S(2)}) copy-start(f32[3,1024]{1,0:T(4,128)S(1)} %collective-permute-done.8) | copy-start | bytes 36868
  68.3 6.1 %collective-permute-start.9 = (f32[3,2048]{1,0:T(4,128)S(1)}, f32[3,2048]{1,0:T(4,128)S(1)}, u32[]{:S(2)}, u32[]{:S(2)}) collective-permute-start(f32[3,2048]{1,0:T(4,128)S(1)} %pad_maximum_fusion.24), channel_id=1, source_target_pairs={{0,30},{1,31},{2,0},{3,1},{4,2},{5,3},{6,4},{7,5},{8,6},{9,7},{10,... | collective-permute-start | bytes 73736 | tf_op jit(solution)/shard_map/ppermute | solution.py:14
  74.4 5.2 %copy-start.11 = (f32[3,2048]{1,0:T(4,128)}, f32[3,2048]{1,0:T(4,128)S(1)}, u32[]{:S(2)}) copy-start(f32[3,2048]{1,0:T(4,128)S(1)} %collective-permute-done.9) | copy-start | bytes 73732
  74.4 5.2 %collective-permute-start.10 = (f32[3,4096]{1,0:T(4,128)S(1)}, f32[3,4096]{1,0:T(4,128)S(1)}, u32[]{:S(2)}, u32[]{:S(2)}) collective-permute-start(f32[3,4096]{1,0:T(4,128)S(1)} %pad_maximum_fusion.23), channel_id=1, source_target_pairs={{0,28},{1,29},{2,30},{3,31},{4,0},{5,1},{6,2},{7,3},{8,4},{9,5},{1... | collective-permute-start | bytes 147464 | tf_op jit(solution)/shard_map/ppermute | solution.py:14
  79.6 6.9 %copy-start.7 = (f32[3,4096]{1,0:T(4,128)}, f32[3,4096]{1,0:T(4,128)S(1)}, u32[]{:S(2)}) copy-start(f32[3,4096]{1,0:T(4,128)S(1)} %collective-permute-done.10) | copy-start | bytes 147460
  79.6 6.2 %collective-permute-start.11 = (f32[3,8192]{1,0:T(4,128)S(1)}, f32[3,8192]{1,0:T(4,128)S(1)}, u32[]{:S(2)}, u32[]{:S(2)}) collective-permute-start(f32[3,8192]{1,0:T(4,128)S(1)} %pad_maximum_fusion.22), channel_id=1, source_target_pairs={{0,24},{1,25},{2,26},{3,27},{4,28},{5,29},{6,30},{7,31},{8,0},{9,1... | collective-permute-start | bytes 294920 | tf_op jit(solution)/shard_map/ppermute | solution.py:14
  85.8 0.7 copy-start.9
  86.6 13.2 %collective-permute-start.12 = (f32[3,16384]{1,0:T(4,128)}, f32[3,16384]{1,0:T(4,128)S(1)}, u32[]{:S(2)}, u32[]{:S(2)}) collective-permute-start(f32[3,16384]{1,0:T(4,128)} %get-tuple-element.20), channel_id=1, source_target_pairs={{0,16},{1,17},{2,18},{3,19},{4,20},{5,21},{6,22},{7,23},{8,24},{9,... | collective-permute-start | bytes 589832 | tf_op jit(solution)/shard_map/ppermute | solution.py:14
  97.2 2.6 copy-start.16
  97.2 2.7 copy-start.14
  97.2 2.7 copy-start.12
  97.2 2.7 copy-start.8
  97.3 2.7 copy-start.10
  100.2 89.3 %copy-start.15 = (f32[3072]{0:T(1024)S(1)}, f32[3072]{0:T(1024)}, u32[]{:S(2)}) copy-start(f32[3072]{0:T(1024)} %fusion.32) | copy-start | bytes 36868
  192.6 4.2 %copy-start.18 = (f32[32,32]{0,1:T(8,128)S(1)}, f32[32,32]{0,1:T(8,128)}, u32[]{:S(2)}) copy-start(f32[32,32]{0,1:T(8,128)} %convolution_bitcast_fusion) | copy-start | bytes 12292
